TPU v7x, 32 devices: a whole 2x2x4 slice. The times are simulated.
32 devices in a mesh: seq: 8 (over z, x), rows: 4 (over y, core).
Axes of the slice: x: 2, y: 2, z: 4, core: 2. Of those that a mesh axis runs over, the one named last changes fastest.
Arguments:
- attn_in: bfloat16 [8192, 8192], P(('seq', 'rows')), may hold values from -6 to 6
- attn_out: bfloat16 [8192, 8192], P(('seq', 'rows')), may hold values from -6 to 6
- valid: int32 [8192], P(('seq', 'rows')), may hold values 0 or 1
- w_qkv: bfloat16 [10240, 8192], P('rows', 'seq'), may hold values from -6 to 6
- w_out: bfloat16 [8192, 8192], P('rows', 'seq'), may hold values from -6 to 6
- qkv_ranks: int32 [10240], P('rows'), may hold values from 3072 to 5120
- out_ranks: int32 [8192], P('rows'), may hold values from 3072 to 5120
Outputs:
- qkv_margins: float32 [10240, 8192], P('rows', 'seq')
- out_margins: float32 [8192, 8192], P('rows', 'seq')
Inputs may be any that keep to these rules, and one draw needn't show every extreme that they name: `qkv_ranks`: each row keeps between three and five eighths of its 8192 weights. `out_ranks`: each row keeps between three and five eighths of its 8192 weights.
All inputs are finite; a program needn't handle non-finite values. No bound on the sum of `valid` on one device may be relied on, other than what follows from the above.
Results may differ from a plain program's by a relative error of at most 0.0003.
Values may be sent and summed in bfloat16 or wider, within the bound.
A program may use at most 128 MiB of HBM per device.

v0:
```python
import jax
import jax.numpy as jnp
from jax import lax
from jax.sharding import PartitionSpec as P

EPS = 1e-06


def tile_scores(weights, norm):
    return jnp.abs(weights.astype(jnp.float32)) * norm[None, :]


def row_limits(scores, ranks):
    lower = jnp.zeros((scores.shape[0],), jnp.float32)
    upper = jnp.max(scores, axis=1) + 1.0

    def bisect(step, state):
        low, high = state
        middle = 0.5 * (low + high)
        counted = jnp.sum((scores >= middle[:, None]).astype(jnp.int32), axis=1)
        rising = counted >= ranks
        return (jnp.where(rising, middle, low), jnp.where(rising, high, middle))

    lower, upper = lax.fori_loop(0, 24, bisect, (lower, upper))
    start = jnp.min(jnp.where(scores >= lower[:, None], scores, jnp.inf), axis=1)

    def strictly_above(candidate):
        return jnp.sum((scores > candidate[:, None]).astype(jnp.int32), axis=1)

    def unfinished(candidate):
        return jnp.any(strictly_above(candidate) >= ranks)

    def advance(candidate):
        further = strictly_above(candidate) >= ranks
        following = jnp.min(jnp.where(scores > candidate[:, None], scores, jnp.inf), axis=1)
        return jnp.where(further, following, candidate)

    return lax.while_loop(unfinished, advance, start)


def clipped(scores, limits):
    return jnp.maximum(scores - limits[:, None], 0.0)


def per_device(attn_in, attn_out, valid, w_qkv, w_out, qkv_ranks, out_ranks):
    weight = valid.astype(jnp.float32)[:, None]

    def squares(acts):
        acts32 = acts.astype(jnp.float32)
        return jnp.sum(acts32 * acts32 * weight, axis=0)

    partial_sums = jnp.stack([squares(attn_in), squares(attn_out)])
    total_tokens = attn_in.shape[0] * lax.axis_size("seq") * lax.axis_size("rows")
    seq_index = lax.axis_index("seq")
    totals = lax.psum(partial_sums, ("seq", "rows"))
    full_norm = jnp.sqrt(totals / total_tokens + EPS)
    qkv_whole, out_whole = (
        lax.all_to_all(w_qkv, "seq", split_axis=0, concat_axis=1, tiled=True),
        lax.all_to_all(w_out, "seq", split_axis=0, concat_axis=1, tiled=True),
    )
    qkv_rows = tile_scores(qkv_whole, full_norm[0])
    out_rows = tile_scores(out_whole, full_norm[1])
    qkv_count = qkv_rows.shape[0]
    out_count = out_rows.shape[0]
    qkv_mine = lax.dynamic_slice_in_dim(qkv_ranks, seq_index * qkv_count, qkv_count)
    out_mine = lax.dynamic_slice_in_dim(out_ranks, seq_index * out_count, out_count)
    qkv_limits = row_limits(qkv_rows, qkv_mine)
    out_limits = row_limits(out_rows, out_mine)
    qkv_result, out_result = (
        lax.all_to_all(
            clipped(qkv_rows, qkv_limits), "seq", split_axis=1, concat_axis=0, tiled=True
        ),
        lax.all_to_all(
            clipped(out_rows, out_limits), "seq", split_axis=1, concat_axis=0, tiled=True
        ),
    )
    return (qkv_result, out_result)


def solution(mesh):
    placed = (
        P(("seq", "rows"), None),
        P(("seq", "rows"), None),
        P(("seq", "rows")),
        P("rows", "seq"),
        P("rows", "seq"),
        P("rows"),
        P("rows"),
    )
    return jax.shard_map(
        per_device,
        mesh=mesh,
        in_specs=placed,
        out_specs=(P("rows", "seq"), P("rows", "seq")),
        check_vma=False,
    )
```

profile of v0, /device:TPU:0, one launch (start us, length us, event | category | flops | bytes accessed | tf_op | source)
XLA Modules:
  0.0 824.9 jit_solution(17134786051954232279)
XLA Ops:
  7.2 7.3 all-to-all-start.2
  14.5 4.7 multiply_reduce_fusion.1
  22.7 165.7 %all-reduce.2.cloned.1.call-done = f32[2,8192]{1,0:T(2,128)} async-done(((f32[2,8192]{1,0:T(2,128)}), f32[2,8192]{1,0:T(2,128)}) %all-reduce.2.cloned.1.call-update) | async-done | bytes 65552 | tf_op jit(solution)/shard_map/psum | solution.py:55
  189.5 5.4 all-to-all-start
  204.4 122.3 %while.43 = (s32[]{:T(128)}, f32[256]{0:T(256)S(1)}, f32[256]{0:T(256)S(1)}, f32[256,8192]{1,0:T(8,128)}, s32[256]{0:T(256)}, /*index=5*/s32[]{:T(128)}, s32[]{:T(128)}) while((s32[]{:T(128)}, f32[256]{0:T(256)S(1)}, f32[256]{0:T(256)S(1)}, f32[256,8192]{1,0:T(8,128)}, s32[256]{0:T(256)}, /*index=5*/s32[]{:T(128)}, ...), condition=%wide.region_17.18_spmd.clone, body=%wide.region_15.17_spmd.clone.sunk | while | flops 6292995 | bytes 8402528 | solution.py:24
  209.5 4.4 convert_reduce_fusion.7
  214.6 4.4 convert_reduce_fusion.7
  326.7 4.5 fusion.10
  331.2 6.6 while.39
  337.8 7.1 fusion.11
  344.9 21.1 %all-to-all-start.3 = ((f32[256,8,1024]{2,0,1:T(8,128)}), f32[256,8,1024]{2,0,1:T(8,128)}, u32[]{:S(2)}, u32[]{:S(2)}) async-start(f32[256,8,1024]{2,0,1:T(8,128)} %fusion.11), calls=%async_computation.3 | async-start | bytes 16777216 | tf_op jit(solution)/shard_map/all_to_all | solution.py:73
  370.2 5.2 copy.11
  375.4 9.7 %broadcast_multiply_fusion = f32[320,8192]{1,0:T(8,128)} fusion(f32[320,8192]{1,0:T(8,128)} %bitcast.30, f32[8192]{0:T(1024)S(1)} %bitcast.34), kind=kLoop, calls=%fused_computation.39 | loop fusion | flops 2621440 | bytes 21004288 | tf_op jit(solution)/shard_map/mul | solution.py:10
  385.0 141.9 %while.42 = (s32[]{:T(128)}, f32[320]{0:T(512)S(1)}, f32[320]{0:T(512)S(1)}, f32[320,8192]{1,0:T(8,128)}, s32[320]{0:T(512)}, /*index=5*/s32[]{:T(128)}, s32[]{:T(128)}) while((s32[]{:T(128)}, f32[320]{0:T(512)S(1)}, f32[320]{0:T(512)S(1)}, f32[320,8192]{1,0:T(8,128)}, s32[320]{0:T(512)}, /*index=5*/s32[]{:T(128)}, s32[]{:T(128)}) %tuple.71), condition=%wide.region_6.7_spmd.clone, body=%wide.region_4.6_spmd.clone.sunk | while | flops 7866243 | bytes 10503136 | solution.py:24
  385.0 5.2 convert_reduce_fusion.6
  391.0 5.2 convert_reduce_fusion.6
  396.9 5.2 convert_reduce_fusion.6
  402.8 5.2 convert_reduce_fusion.6
  408.7 5.2 convert_reduce_fusion.6
  414.6 5.2 convert_reduce_fusion.6
  420.5 5.2 convert_reduce_fusion.6
  426.4 5.2 convert_reduce_fusion.6
  432.4 5.2 convert_reduce_fusion.6
  438.3 5.2 convert_reduce_fusion.6
  444.2 5.2 convert_reduce_fusion.6
  450.1 5.2 convert_reduce_fusion.6
  456.0 5.2 convert_reduce_fusion.6
  461.9 5.2 convert_reduce_fusion.6
  467.8 5.2 convert_reduce_fusion.6
  473.7 5.2 convert_reduce_fusion.6
  479.7 5.2 convert_reduce_fusion.6
  485.6 5.2 convert_reduce_fusion.6
  491.5 5.2 convert_reduce_fusion.6
  497.4 5.2 convert_reduce_fusion.6
  503.3 5.2 convert_reduce_fusion.6
  509.2 5.2 convert_reduce_fusion.6
  515.1 5.2 convert_reduce_fusion.6
  521.0 5.2 convert_reduce_fusion.6
  526.9 5.3 fusion.5
  532.2 24.8 %while.37 = (f32[320]{0:T(512)}, f32[320,8192]{1,0:T(8,128)}, s32[320]{0:T(512)}) while((f32[320]{0:T(512)}, f32[320,8192]{1,0:T(8,128)}, s32[320]{0:T(512)}) %tuple.87), condition=%region_11.14_spmd, body=%region_8.11_spmd | while | flops 23593280 | bytes 73417016 | solution.py:38
  532.2 5.2 convert_reduce_fusion
  539.6 5.3 fusion.1
  549.8 5.2 convert_reduce_fusion
  557.0 8.4 %fusion.6 = f32[320,8,1024]{2,0,1:T(8,128)} fusion(bf16[8,320,1024]{2,1,0:T(8,128)(2,1)} %all-to-all-done, f32[320]{0:T(512)} %get-tuple-element.95, f32[8,1024]{1,0:T(8,128)S(1)} %mul.81), kind=kLoop, calls=%fused_computation.25 | loop fusion | flops 13107200 | bytes 15762688 | tf_op jit(solution)/shard_map/max | solution.py:42
  565.4 5.1 all-to-all-start.1
  570.6 228.8 %all-to-all-done.1 = f32[320,8,1024]{2,0,1:T(8,128)} async-done(((f32[320,8,1024]{2,0,1:T(8,128)}), f32[320,8,1024]{2,0,1:T(8,128)}, u32[]{:S(2)}, u32[]{:S(2)}) %all-to-all-start.1) | async-done | bytes 10485792 | tf_op jit(solution)/shard_map/all_to_all | solution.py:70
  799.4 10.3 %copy.40 = f32[2560,1024]{1,0:T(8,128)} copy(f32[2560,1024]{1,0:T(8,128)} %bitcast.7) | data formatting | bytes 20971520
  809.6 8.4 %copy.41 = f32[2048,1024]{1,0:T(8,128)} copy(f32[2048,1024]{1,0:T(8,128)} %bitcast.13) | data formatting | bytes 16777216
  (197 shorter events, 161.7 us)
Async XLA Ops:
  7.2 7.4 copy-start.2
  7.2 182.3 %all-to-all-start.2 = ((bf16[8,256,1024]{2,1,0:T(8,128)(2,1)}), bf16[8,256,1024]{2,1,0:T(8,128)(2,1)}, u32[]{:S(2)}, u32[]{:S(2)}) async-start(bf16[8,256,1024]{2,1,0:T(8,128)(2,1)} %bitcast.33), calls=%async_computation.2 | async-start | bytes 8388608 | tf_op jit(solution)/shard_map/all_to_all | solution.py:59
  14.5 173.9 %all-reduce.2.cloned.1.call-start = ((), (), s32[]{:S(2)}) async-start(), calls=%async_computation.4 | async-start | bytes 131072 | tf_op jit(solution)/shard_map/psum | solution.py:55
  189.5 155.4 %all-to-all-start = ((bf16[8,320,1024]{2,1,0:T(8,128)(2,1)}), bf16[8,320,1024]{2,1,0:T(8,128)(2,1)}, u32[]{:S(2)}, u32[]{:S(2)}) async-start(bf16[8,320,1024]{2,1,0:T(8,128)(2,1)} %bitcast.32), calls=%async_computation | async-start | bytes 10485760 | tf_op jit(solution)/shard_map/all_to_all | solution.py:58
  344.9 220.5 %all-to-all-start.3 = ((f32[256,8,1024]{2,0,1:T(8,128)}), f32[256,8,1024]{2,0,1:T(8,128)}, u32[]{:S(2)}, u32[]{:S(2)}) async-start(f32[256,8,1024]{2,0,1:T(8,128)} %fusion.11), calls=%async_computation.3 | async-start | bytes 16777216 | tf_op jit(solution)/shard_map/all_to_all | solution.py:73
  539.6 7.0 copy-start
  565.4 233.9 %all-to-all-start.1 = ((f32[320,8,1024]{2,0,1:T(8,128)}), f32[320,8,1024]{2,0,1:T(8,128)}, u32[]{:S(2)}, u32[]{:S(2)}) async-start(f32[320,8,1024]{2,0,1:T(8,128)} %fusion.6), calls=%async_computation.1 | async-start | bytes 20971520 | tf_op jit(solution)/shard_map/all_to_all | solution.py:70
Sparse Core Ops, SparseCore 0:
  21.4 166.8 all-reduce.1
where the time goes:
time: 829 us; the launch traced here: 825 us
  waiting for transfers between devices  394 us (48%)
  other arithmetic  344 us (41%)
  starting transfers between devices  39 us (5%)
  local copies, waits for them, and re-layouts  30.1 us (4%)
  between operations  14.2 us (2%)
    reduce_sum x48, other arithmetic, bisect(): counted = jnp.sum((scores >= middle[:, None]).astype(jnp.int32), axis=1)  229 us
    all_to_all x1, waiting for transfers between devices, per_device(): lax.all_to_all(clipped(qkv_rows, qkv_limits), 'seq', split_axis=1, concat...  229 us
    psum x1, waiting for transfers between devices, per_device(): totals = lax.psum(partial_sums, ('seq', 'rows'))  166 us
    select_n x96, other arithmetic, bisect(): return (jnp.where(rising, middle, low), jnp.where(rising, high, middle))  33.9 us
    all_to_all x1, starting transfers between devices, per_device(): lax.all_to_all(clipped(out_rows, out_limits), 'seq', split_axis=1, concat...  21.1 us
    unnamed x4, local copies, waits for them, and re-layouts  18.7 us
    reduce_sum x4, other arithmetic, strictly_above(): return jnp.sum((scores > candidate[:, None]).astype(jnp.int32), axis=1)  16.6 us
  transfers between devices with their start and end apart: 5, of which 2 were waited for; matrix products, arithmetic and copies ran while one was open for 43% of the time, Pallas kernels for 0%

commit v1 on v0

--- a/solution.py
+++ b/solution.py
@@ -52,7 +52,7 @@
     partial_sums = jnp.stack([squares(attn_in), squares(attn_out)])
     total_tokens = attn_in.shape[0] * lax.axis_size("seq") * lax.axis_size("rows")
     seq_index = lax.axis_index("seq")
-    totals = lax.psum(partial_sums, ("seq", "rows"))
+    totals = jnp.sum(lax.all_gather(partial_sums, ("seq", "rows")), axis=0)
     full_norm = jnp.sqrt(totals / total_tokens + EPS)
     qkv_whole, out_whole = (
         lax.all_to_all(w_qkv, "seq", split_axis=0, concat_axis=1, tiled=True),

time: 829 us -> 770 us (0.929)
  waiting for transfers between devices: 394 us -> 335 us
    psum x1 -> x0, waiting for transfers between devices: 166 us -> none  [per_device(): totals = lax.psum(partial_sums, ('seq', 'rows'))]
    all_gather x0 -> x1, waiting for transfers between devices: none -> 109 us  [per_device(): totals = jnp.sum(lax.all_gather(partial_sums, ('seq', 'rows')), axis=0)]
  transfers between devices with their start and end apart: 5 -> 5, of which waited for: 2 -> 2; matrix products, arithmetic and copies ran while one was open for 43% -> 46% of each run, Pallas kernels for 0% -> 0%
where the time goes in v1:
time: 770 us; the launch traced here: 766 us
  other arithmetic  345 us (45%)
  waiting for transfers between devices  335 us (44%)
  starting transfers between devices  38.2 us (5%)
  local copies, waits for them, and re-layouts  30.1 us (4%)
  between operations  14.2 us (2%)
    reduce_sum x48, other arithmetic, bisect(): counted = jnp.sum((scores >= middle[:, None]).astype(jnp.int32), axis=1)  229 us
    all_to_all x1, waiting for transfers between devices, per_device(): lax.all_to_all(clipped(qkv_rows, qkv_limits), 'seq', split_axis=1, concat...  226 us
    all_gather x1, waiting for transfers between devices, per_device(): totals = jnp.sum(lax.all_gather(partial_sums, ('seq', 'rows')), axis=0)  109 us
    select_n x96, other arithmetic, bisect(): return (jnp.where(rising, middle, low), jnp.where(rising, high, middle))  33.9 us
    all_to_all x1, starting transfers between devices, per_device(): lax.all_to_all(clipped(out_rows, out_limits), 'seq', split_axis=1, concat...  21.1 us
    unnamed x4, local copies, waits for them, and re-layouts  18.7 us
    reduce_sum x4, other arithmetic, strictly_above(): return jnp.sum((scores > candidate[:, None]).astype(jnp.int32), axis=1)  16.6 us
    max x2, other arithmetic, clipped(): return jnp.maximum(scores - limits[:, None], 0.0)  15.6 us
  transfers between devices with their start and end apart: 5, of which 2 were waited for; matrix products, arithmetic and copies ran while one was open for 46% of the time, Pallas kernels for 0%

profile of v1, /device:TPU:0, one launch (start us, length us, event | category | flops | bytes accessed | tf_op | source)
XLA Modules:
  0.0 766.0 jit_solution(8481517645163915200)
XLA Ops:
  7.2 7.3 all-to-all-start.2
  14.5 4.7 multiply_reduce_fusion.1
  22.7 109.1 %all-gather.4.cloned.1.call-done = f32[32,2,8192]{2,1,0:T(2,128)} async-done(((f32[1,2,8192]{2,1,0:T(2,128)}), f32[32,2,8192]{2,1,0:T(2,128)}) %all-gather.4.cloned.1.call-update) | async-done | bytes 2097168 | tf_op jit(solution)/shard_map/all_gather | solution.py:55
  134.5 4.7 all-to-all-start
  148.6 122.3 %while.43 = (s32[]{:T(128)}, f32[256]{0:T(256)S(1)}, f32[256]{0:T(256)S(1)}, f32[256,8192]{1,0:T(8,128)}, s32[256]{0:T(256)}, /*index=5*/s32[]{:T(128)}, s32[]{:T(128)}) while((s32[]{:T(128)}, f32[256]{0:T(256)S(1)}, f32[256]{0:T(256)S(1)}, f32[256,8192]{1,0:T(8,128)}, s32[256]{0:T(256)}, /*index=5*/s32[]{:T(128)}, ...), condition=%wide.region_17.18_spmd.clone, body=%wide.region_15.17_spmd.clone.sunk | while | flops 6292995 | bytes 8402528 | solution.py:24
  153.7 4.4 convert_reduce_fusion.7
  163.9 4.4 convert_reduce_fusion.7
  270.9 4.5 fusion.10
  275.4 6.6 while.39
  282.0 7.1 fusion.11
  289.1 21.1 %all-to-all-start.3 = ((f32[256,8,1024]{2,0,1:T(8,128)}), f32[256,8,1024]{2,0,1:T(8,128)}, u32[]{:S(2)}, u32[]{:S(2)}) async-start(f32[256,8,1024]{2,0,1:T(8,128)} %fusion.11), calls=%async_computation.3 | async-start | bytes 16777216 | tf_op jit(solution)/shard_map/all_to_all | solution.py:73
  314.3 5.2 copy.13
  319.5 9.7 %broadcast_multiply_fusion = f32[320,8192]{1,0:T(8,128)} fusion(f32[320,8192]{1,0:T(8,128)} %bitcast.32, f32[8192]{0:T(1024)S(1)} %bitcast.36), kind=kLoop, calls=%fused_computation.39 | loop fusion | flops 2621440 | bytes 21004288 | tf_op jit(solution)/shard_map/mul | solution.py:10
  329.2 141.9 %while.42 = (s32[]{:T(128)}, f32[320]{0:T(512)S(1)}, f32[320]{0:T(512)S(1)}, f32[320,8192]{1,0:T(8,128)}, s32[320]{0:T(512)}, /*index=5*/s32[]{:T(128)}, s32[]{:T(128)}) while((s32[]{:T(128)}, f32[320]{0:T(512)S(1)}, f32[320]{0:T(512)S(1)}, f32[320,8192]{1,0:T(8,128)}, s32[320]{0:T(512)}, /*index=5*/s32[]{:T(128)}, s32[]{:T(128)}) %tuple.71), condition=%wide.region_6.7_spmd.clone, body=%wide.region_4.6_spmd.clone.sunk | while | flops 7866243 | bytes 10503136 | solution.py:24
  329.2 5.2 convert_reduce_fusion.6
  335.1 5.2 convert_reduce_fusion.6
  341.0 5.2 convert_reduce_fusion.6
  346.9 5.2 convert_reduce_fusion.6
  352.8 5.2 convert_reduce_fusion.6
  358.7 5.2 convert_reduce_fusion.6
  364.6 5.2 convert_reduce_fusion.6
  370.6 5.2 convert_reduce_fusion.6
  376.5 5.2 convert_reduce_fusion.6
  382.4 5.2 convert_reduce_fusion.6
  388.3 5.2 convert_reduce_fusion.6
  394.2 5.2 convert_reduce_fusion.6
  400.1 5.2 convert_reduce_fusion.6
  406.0 5.2 convert_reduce_fusion.6
  411.9 5.2 convert_reduce_fusion.6
  417.9 5.2 convert_reduce_fusion.6
  423.8 5.2 convert_reduce_fusion.6
  429.7 5.2 convert_reduce_fusion.6
  435.6 5.2 convert_reduce_fusion.6
  441.5 5.2 convert_reduce_fusion.6
  447.4 5.2 convert_reduce_fusion.6
  453.3 5.2 convert_reduce_fusion.6
  459.2 5.2 convert_reduce_fusion.6
  465.2 5.2 convert_reduce_fusion.6
  471.1 5.3 fusion.5
  476.3 24.8 %while.37 = (f32[320]{0:T(512)}, f32[320,8192]{1,0:T(8,128)}, s32[320]{0:T(512)}) while((f32[320]{0:T(512)}, f32[320,8192]{1,0:T(8,128)}, s32[320]{0:T(512)}) %tuple.87), condition=%region_11.14_spmd, body=%region_8.11_spmd | while | flops 23593280 | bytes 73417016 | solution.py:38
  476.3 5.2 convert_reduce_fusion
  483.5 5.3 fusion.1
  493.6 5.2 convert_reduce_fusion
  501.1 8.4 %fusion.6 = f32[320,8,1024]{2,0,1:T(8,128)} fusion(bf16[8,320,1024]{2,1,0:T(8,128)(2,1)} %all-to-all-done, f32[320]{0:T(512)} %get-tuple-element.95, f32[8,1024]{1,0:T(8,128)S(1)} %mul.81), kind=kLoop, calls=%fused_computation.25 | loop fusion | flops 13107200 | bytes 15762688 | tf_op jit(solution)/shard_map/max | solution.py:42
  509.5 5.1 all-to-all-start.1
  514.7 225.8 %all-to-all-done.1 = f32[320,8,1024]{2,0,1:T(8,128)} async-done(((f32[320,8,1024]{2,0,1:T(8,128)}), f32[320,8,1024]{2,0,1:T(8,128)}, u32[]{:S(2)}, u32[]{:S(2)}) %all-to-all-start.1) | async-done | bytes 10485792 | tf_op jit(solution)/shard_map/all_to_all | solution.py:70
  740.5 10.3 %copy.41 = f32[2560,1024]{1,0:T(8,128)} copy(f32[2560,1024]{1,0:T(8,128)} %bitcast.8) | data formatting | bytes 20971520
  750.8 8.4 %copy.42 = f32[2048,1024]{1,0:T(8,128)} copy(f32[2048,1024]{1,0:T(8,128)} %bitcast.14) | data formatting | bytes 16777216
  (198 shorter events, 163.2 us)
Async XLA Ops:
  7.2 7.4 copy-start.2
  7.2 127.3 %all-to-all-start.2 = ((bf16[8,256,1024]{2,1,0:T(8,128)(2,1)}), bf16[8,256,1024]{2,1,0:T(8,128)(2,1)}, u32[]{:S(2)}, u32[]{:S(2)}) async-start(bf16[8,256,1024]{2,1,0:T(8,128)(2,1)} %bitcast.35), calls=%async_computation.2 | async-start | bytes 8388608 | tf_op jit(solution)/shard_map/all_to_all | solution.py:59
  14.5 117.4 %all-gather.4.cloned.1.call-start = ((), (), s32[]{:S(2)}) async-start(), calls=%async_computation.4 | async-start | bytes 2162688 | tf_op jit(solution)/shard_map/all_gather | solution.py:55
  134.5 154.7 %all-to-all-start = ((bf16[8,320,1024]{2,1,0:T(8,128)(2,1)}), bf16[8,320,1024]{2,1,0:T(8,128)(2,1)}, u32[]{:S(2)}, u32[]{:S(2)}) async-start(bf16[8,320,1024]{2,1,0:T(8,128)(2,1)} %bitcast.34), calls=%async_computation | async-start | bytes 10485760 | tf_op jit(solution)/shard_map/all_to_all | solution.py:58
  289.1 220.4 %all-to-all-start.3 = ((f32[256,8,1024]{2,0,1:T(8,128)}), f32[256,8,1024]{2,0,1:T(8,128)}, u32[]{:S(2)}, u32[]{:S(2)}) async-start(f32[256,8,1024]{2,0,1:T(8,128)} %fusion.11), calls=%async_computation.3 | async-start | bytes 16777216 | tf_op jit(solution)/shard_map/all_to_all | solution.py:73
  483.5 7.0 copy-start
  509.5 231.0 %all-to-all-start.1 = ((f32[320,8,1024]{2,0,1:T(8,128)}), f32[320,8,1024]{2,0,1:T(8,128)}, u32[]{:S(2)}, u32[]{:S(2)}) async-start(f32[320,8,1024]{2,0,1:T(8,128)} %fusion.6), calls=%async_computation.1 | async-start | bytes 20971520 | tf_op jit(solution)/shard_map/all_to_all | solution.py:70
Sparse Core Ops, SparseCore 0:
  20.1 111.7 all-gather.3
